TPU v7x, 32 devices: a whole 2x2x4 slice. The times are simulated.
32 devices in a mesh: tm: 8 (over z, y), space: 4 (over x, core).
Axes of the slice: x: 2, y: 2, z: 4, core: 2. Of those that a mesh axis runs over, the one named last changes fastest.
Arguments:
- density: bfloat16 [2048, 128, 128], P('tm', 'space'), may hold values from -6 to 6
- active: int32 [2048], P('tm'), may hold values from 1 to 128
- neighbours: int32 [128, 8], P('space'), may hold values from 0 to 127, as said below
- near_blocks: bfloat16 [2, 128, 8, 128, 128], P(None, 'space'), may hold values from -0.125 to 0.125
- to_moments: bfloat16 [64, 128, 128], P(None, 'space'), may hold values from -0.046875 to 0.046875
- from_moments: bfloat16 [64, 128, 128], P(None, 'space'), may hold values from -0.75 to 0.75
- decay_rates: float32 [64], replicated, may hold values from 9.765625e-05 to 0.05, as said below
- lengths: float32 [2048], P('tm'), may hold values from 0.5 to 1024, as said below
Outputs:
- potential: bfloat16 [2048, 128, 128], P('tm', 'space')
Inputs may be any that keep to these rules, and one draw needn't show every extreme that they name: `neighbours`: every entry of row c lies within 8 of c; each row names c - 8 and c + 8, clipped to the clusters that exist. `decay_rates`: positive rates. Positive lengths.
All inputs are finite; a program needn't handle non-finite values.
Results may differ from a plain program's by a relative error of at most 0.0085.
Values may be sent and summed in bfloat16 or wider, within the bound.
A program may use at most 128 MiB of HBM per device.

v0:
```python
import jax
import jax.numpy as jnp
from jax import lax
from jax.sharding import PartitionSpec as P

REACH = 8


def shifted(block, axis, distance):
    devices = range(lax.axis_size(axis))
    route = [(i - distance, i) for i in devices if i - distance in devices]
    return lax.ppermute(block, axis, route)


def extended_2(block, sides, width):
    for axis, dim in sides:
        count = lax.axis_size(axis)
        forward = [(i, i + 1) for i in range(count - 1)]
        backward = [(target, source) for source, target in forward]
        low = lax.ppermute(
            lax.slice_in_dim(block, block.shape[dim] - width, None, axis=dim), axis, forward
        )
        high = lax.ppermute(lax.slice_in_dim(block, 0, width, axis=dim), axis, backward)
        block = jnp.concatenate([low, block, high], axis=dim)
    return block


def prefix_2(x, axis, combine, identity):
    peers, place = (lax.axis_size(axis), lax.axis_index(axis))
    everything = jax.tree.map(lambda part: lax.all_gather(part, axis), x)
    start = jax.tree.map(
        lambda part, zero: jnp.broadcast_to(jnp.asarray(zero, part.dtype), part.shape), x, identity
    )

    def lap(k, before):
        reached = k < place
        new = combine(before, jax.tree.map(lambda part: part[k], everything))
        return jax.tree.map(lambda a, b: jnp.where(reached, a, b), new, before)

    return lax.fori_loop(0, peers, lap, start)


def combine(earlier, later):
    return (earlier[0] * later[0], later[0] * earlier[1] + later[1])


def slab_terms(rates, moments, lengths):
    steps_here = lengths.shape[0]
    inclusive = jnp.cumsum(lengths)
    exclusive = inclusive - lengths
    spread = jnp.maximum(exclusive[:, None] - inclusive[None, :], 0.0)
    positions = jnp.arange(steps_here, dtype=jnp.int32)
    before_mask = positions[None, :] < positions[:, None]
    weights = jnp.where(
        before_mask[None, :, :], jnp.exp(-rates[:, None, None] * spread[None, :, :]), 0.0
    )
    local_far = jnp.einsum("mts,sm->tm", weights, moments, precision=lax.Precision.HIGHEST)
    total_decay = jnp.exp(-rates * inclusive[-1])
    end_weights = jnp.exp(-rates[None, :] * (inclusive[-1] - inclusive)[:, None])
    end_state = jnp.sum(end_weights * moments, axis=0)
    return (local_far, end_state, total_decay, exclusive)


def local(density, active, neighbours, near_blocks, to_moments, from_moments, decay_rates, lengths):
    steps_here, clusters_here, unknowns = density.shape
    blocks_each = neighbours.shape[1]
    space_index = lax.axis_index("space")
    first_cluster = space_index * clusters_here
    global_ids = first_cluster + jnp.arange(clusters_here, dtype=jnp.int32)
    live_mask = (global_ids[None, :] < active[:, None]).astype(jnp.bfloat16)
    masked = density * live_mask[:, :, None]
    last_row = shifted(masked[-1:], "tm", 1)
    extended = jnp.concatenate([last_row, masked], 0)
    window = extended_2(extended, (("space", 1),), REACH)
    cluster_major = jnp.transpose(window, (1, 0, 2))
    local_index = (neighbours - (first_cluster - REACH)).reshape(-1)
    picked = jnp.take(cluster_major, local_index, axis=0).reshape(
        clusters_here, blocks_each, steps_here + 1, unknowns
    )
    both_lags = jnp.einsum(
        "cjte,lcjef->ctlf", picked, near_blocks, preferred_element_type=jnp.float32
    )
    near_term = both_lags[:, 1:, 0, :] + both_lags[:, :-1, 1, :]
    near_term = jnp.transpose(near_term, (1, 0, 2))
    terms = decay_rates.shape[0]
    share_width = terms // lax.axis_size("space")
    flat = masked.reshape(steps_here, clusters_here * unknowns)
    partial_moments = lax.dot_general(
        flat,
        to_moments.reshape(terms, clusters_here * unknowns),
        (((1,), (1,)), ((), ())),
        preferred_element_type=jnp.float32,
    )
    moments = lax.psum_scatter(
        partial_moments.astype(jnp.bfloat16), "space", scatter_dimension=1, tiled=True
    ).astype(jnp.float32)
    rates_here = lax.dynamic_slice_in_dim(decay_rates, space_index * share_width, share_width)
    local_far, end_state, total_decay, exclusive = slab_terms(rates_here, moments, lengths)
    prefix = prefix_2(
        (total_decay, end_state),
        "tm",
        combine,
        (jnp.ones_like(total_decay), jnp.zeros_like(end_state)),
    )
    arriving = prefix[1]
    far_coeff = jnp.exp(-rates_here[None, :] * exclusive[:, None]) * arriving[None, :] + local_far
    scaled = (far_coeff * jnp.sqrt(2.0 * rates_here)[None, :]).astype(jnp.bfloat16)
    scaled = lax.all_gather(scaled, "space", axis=1, tiled=True)
    far_term = jnp.dot(
        scaled,
        from_moments.reshape(terms, clusters_here * unknowns),
        preferred_element_type=jnp.float32,
    )
    far_term = far_term.reshape(steps_here, clusters_here, unknowns)
    return (live_mask.astype(jnp.float32)[:, :, None] * (near_term + far_term)).astype(jnp.bfloat16)


def solution(mesh):
    placed = (
        P("tm", "space", None),
        P("tm"),
        P("space", None),
        P(None, "space", None, None, None),
        P(None, "space", None),
        P(None, "space", None),
        P(),
        P("tm"),
    )
    return jax.shard_map(
        local, mesh=mesh, in_specs=placed, out_specs=P("tm", "space", None), check_vma=False
    )
```

profile of v0, /device:TPU:0, one launch (start us, length us, event | category | flops | bytes accessed | tf_op | source)
XLA Modules:
  0.0 120.6 jit_solution(849200026766701892)
XLA Ops:
  6.6 0.8 fusion.31
  7.4 3.2 %copy_multiply_fusion = bf16[256,32,128]{2,0,1:T(8,128)(2,1)S(1)} fusion(bf16[256,32,128]{2,1,0:T(8,128)(2,1)} %param.10, bf16[256,32]{0,1:T(8,128)(2,1)S(1)} %get-tuple-element.139), kind=kLoop, calls=%fused_computation.22 | loop fusion | flops 1048576 | bytes 4210688 | tf_op jit(solution)/shard_map/mul | solution.py:71
  10.7 4.9 %collective-permute-start = (bf16[1,32,128]{2,0,1:T(2,128)(2,1)S(1)}, bf16[1,32,128]{2,0,1:T(2,128)(2,1)S(1)}, u32[]{:S(2)}, u32[]{:S(2)}) collective-permute-start(bf16[1,32,128]{2,0,1:T(2,128)(2,1)S(1)} %slice.36), channel_id=1, source_target_pairs={{0,4},{4,8},{8,12},{12,16},{16,20},{20,24},{24,28},{1,5},{5,9},{9,... | collective-permute-start | bytes 24584 | tf_op jit(solution)/shard_map/ppermute | solution.py:12
  15.6 1.4 %fusion.23 = bf16[256,64]{0,1:T(8,128)(2,1)} fusion(bf16[256,32,128]{2,0,1:T(8,128)(2,1)S(1)} %copy_multiply_fusion, bf16[64,32,128]{2,1,0:T(8,128)(2,1)S(1)} %copy-done), kind=kOutput, calls=%fused_computation.28 | convolution fusion | flops 134234112 | bytes 2654208 | tf_op jit(solution)/shard_map/dot_general | solution.py:88
  17.7 0.6 slice.33
  18.3 0.6 broadcast_subtract_fusion.1
  20.5 1.3 %exponential_dynamic-update-slice_fusion = (f32[128]{0:T(128)S(1)}, f32[16]{0:T(128)S(1)}, f32[16]{0:T(128)}) fusion(f32[128]{0:T(128)S(1)} %broadcast.121.clone, u32[]{:T(128)} %bitcast.12, f32[]{:T(128)} %bitcast.11, f32[64]{0:T(128)S(1)} %copy-done.3, s32[]{:T(128)S(6)} %select_n.54), kind=kLoop, calls=%fused_computation.54 | loop fusion | flops 48 | bytes 1164
  22.5 0.9 copy.26
  23.4 1.3 %collective-permute-start.2 = (bf16[257,8,128]{2,1,0:T(8,128)(2,1)}, bf16[257,8,128]{2,1,0:T(8,128)(2,1)}, u32[]{:S(2)}, u32[]{:S(2)}) collective-permute-start(bf16[257,8,128]{2,1,0:T(8,128)(2,1)} %copy.26), channel_id=1, source_target_pairs={{1,0},{2,1},{3,2},{5,4},{6,5},{7,6},{9,8},{10,9},{11,10},{13,12},{... | collective-permute-start | bytes 1579016 | tf_op jit(solution)/shard_map/ppermute | solution.py:23
  24.6 3.8 %collective-permute-start.1 = (bf16[257,8,128]{2,1,0:T(8,128)(2,1)S(1)}, bf16[257,8,128]{2,1,0:T(8,128)(2,1)}, u32[]{:S(2)}, u32[]{:S(2)}) collective-permute-start(bf16[257,8,128]{2,1,0:T(8,128)(2,1)S(1)} %copy.25), channel_id=1, source_target_pairs={{0,1},{1,2},{2,3},{4,5},{5,6},{6,7},{8,9},{9,10},{10,11},{12,13},{... | collective-permute-start | bytes 1579016 | tf_op jit(solution)/shard_map/ppermute | solution.py:20
  28.5 8.5 %reduce-scatter.2.cloned.1.call-done = bf16[256,16]{0,1:T(8,128)(2,1)} async-done(((bf16[256,64]{0,1:T(8,128)(2,1)}), bf16[256,16]{0,1:T(8,128)(2,1)}) %reduce-scatter.2.cloned.1.call-update) | async-done | bytes 8208 | tf_op jit(solution)/shard_map/reduce_scatter | solution.py:94
  37.0 0.9 multiply_reduce_fusion
  38.6 22.0 %all-reduce.2 = (f32[128]{0:T(128)S(1)}, f32[128]{0:T(128)}) all-reduce(f32[128]{0:T(128)} %copy-done.5, f32[128]{0:T(128)} %copy-done.7), channel_id=2, replica_groups=mesh['tm'=8,'space'=4] {'tm'}, use_global_device_ids=true, to_apply=%add | all-reduce | flops 256 | bytes 2048
  60.7 0.7 reshape.200
  61.8 3.3 %fusion.10 = f32[16,1,256]{2,1,0:T(1,128)S(1)} fusion(f32[256,256]{1,0:T(8,128)S(1)} %subtract_maximum_fusion, f32[16]{0:T(128)S(1)} %get-tuple-element.131, pred[256,256]{1,0:T(8,128)(4,1)S(1)} %iota_compare_fusion, bf16[256,16,1]{0,1,2:T(8,128)(2,1)} %bitcast.73), kind=kOutput, calls=%fused_computation.16 | convolution fusion | flops 14680064 | bytes 352320 | tf_op jit(solution)/shard_map/mts,sm->tm/dot_general | solution.py:57
  65.1 0.7 fusion.29
  65.8 5.4 %all_gather.19 = bf16[256,64]{0,1:T(8,128)(2,1)S(1)} all-gather(bf16[256,16]{0,1:T(8,128)(2,1)S(1)} %fusion.29), channel_id=1, replica_groups=mesh['tm'=8,'space'=4] {'space'}, dimensions={1}, use_global_device_ids=true | all-gather | bytes 40960 | tf_op jit(solution)/shard_map/all_gather | solution.py:108
  71.2 1.1 copy.28
  72.4 1.1 copy.27
  73.5 4.2 %maximum_bitcast_fusion = bf16[48,257,128]{2,1,0:T(8,128)(2,1)} fusion(bf16[257,8,128]{2,0,1:T(8,128)(2,1)S(1)} %copy.28, bf16[256,32,128]{2,0,1:T(8,128)(2,1)S(1)} %copy_multiply_fusion, bf16[1,32,128]{2,0,1:T(2,128)(2,1)S(1)} %collective-permute-done, bf16[257,8,128]{2,0,1:T(8,128)(2,1)S(1)} %copy.27), kind=kLoop, calls=%fused_computation.21 | loop fusion | flops 12632064 | bytes 6316032 | tf_op jit(solution)/shard_map/transpose | solution.py:75
  77.6 12.1 %gather_fusion = bf16[256,257,128]{2,1,0:T(8,128)(2,1)} fusion(bf16[48,257,128]{2,1,0:T(8,128)(2,1)} %maximum_bitcast_fusion, s32[1024]{0:T(1024)S(1)} %pad_clamp_fusion), kind=kCustom, calls=%fused_computation | custom fusion | bytes 33686528 | tf_op jit(solution)/shard_map/jit(_take)/gather | solution.py:77
  89.8 16.8 %fusion.14 = f32[32,257,2,128]{3,1,2,0:T(8,128)} fusion(bf16[2,32,8,128,128]{4,3,2,1,0:T(8,128)(2,1)} %param.13, bf16[32,8,257,128]{3,2,1,0:T(8,128)(2,1)} %bitcast.72, pred[32,8]{1,0:T(8,128)(4,1)S(1)} %copy.23), kind=kOutput, calls=%fused_computation.20 | convolution fusion | flops 4320165888 | bytes 42041600 | tf_op jit(solution)/shard_map/cjte,lcjef->ctlf/dot_general | solution.py:80
  106.6 4.4 %fusion.9 = bf16[256,32,128]{2,0,1:T(8,128)(2,1)S(1)} fusion(f32[32,257,2,128]{3,1,2,0:T(8,128)} %fusion.14, f32[256,32]{0,1:T(8,128)S(1)} %get-tuple-element.138, bf16[256,64]{0,1:T(8,128)(2,1)S(1)} %all_gather.19, bf16[8,8,32,128]{3,2,1,0:T(8,128)(2,1)S(1)} %bitcast.76), kind=kOutput, calls=%fused_computation.15 | convolution fusion | flops 138412032 | bytes 11075584 | tf_op jit(solution)/shard_map/dot_general | solution.py:109
  111.1 2.7 %copy.33 = bf16[256,32,128]{2,1,0:T(8,128)(2,1)} copy(bf16[256,32,128]{2,0,1:T(8,128)(2,1)S(1)} %fusion.9) | data formatting | bytes 4194304 | tf_op jit(solution)/shard_map/convert_element_type | solution.py:115
  (53 shorter events, 3.5 us)
Async XLA Ops:
  6.5 9.1 %copy-start = (bf16[64,32,128]{2,1,0:T(8,128)(2,1)S(1)}, bf16[64,32,128]{2,1,0:T(8,128)(2,1)}, u32[]{:S(2)}) copy-start(bf16[64,32,128]{2,1,0:T(8,128)(2,1)} %param.14) | copy-start | bytes 1572868
  6.5 12.7 %copy-start.6 = (u32[32]{0:T(128)S(1)}, u32[32]{0:T(128)}, u32[]{:S(2)}) copy-start(u32[32]{0:T(128)} %constant.68) | copy-start | bytes 388
  6.5 10.5 %copy-start.2 = (f32[256]{0:T(256)S(1)}, f32[256]{0:T(256)}, u32[]{:S(2)}) copy-start(f32[256]{0:T(256)} %param.17) | copy-start | bytes 3076
  6.5 12.4 %copy-start.1 = (s32[32,8]{0,1:T(8,128)S(1)}, s32[32,8]{0,1:T(8,128)}, u32[]{:S(2)}) copy-start(s32[32,8]{0,1:T(8,128)} %param.12) | copy-start | bytes 3076
  6.5 14.0 %copy-start.3 = (f32[64]{0:T(128)S(1)}, f32[64]{0:T(128)}, u32[]{:S(2)}) copy-start(f32[64]{0:T(128)} %param.16) | copy-start | bytes 772
  6.5 30.4 %reduce-scatter.2.cloned.1.call-start = ((), (), s32[]{:S(2)}) async-start(), calls=%async_computation.1 | async-start | bytes 40960 | tf_op jit(solution)/shard_map/reduce_scatter | solution.py:94
  10.7 11.2 %collective-permute-start = (bf16[1,32,128]{2,0,1:T(2,128)(2,1)S(1)}, bf16[1,32,128]{2,0,1:T(2,128)(2,1)S(1)}, u32[]{:S(2)}, u32[]{:S(2)}) collective-permute-start(bf16[1,32,128]{2,0,1:T(2,128)(2,1)S(1)} %slice.36), channel_id=1, source_target_pairs={{0,4},{4,8},{8,12},{12,16},{16,20},{20,24},{24,28},{1,5},{5,9},{9,... | collective-permute-start | bytes 24584 | tf_op jit(solution)/shard_map/ppermute | solution.py:12
  21.8 0.6 copy-start.5
  23.4 47.9 %collective-permute-start.2 = (bf16[257,8,128]{2,1,0:T(8,128)(2,1)}, bf16[257,8,128]{2,1,0:T(8,128)(2,1)}, u32[]{:S(2)}, u32[]{:S(2)}) collective-permute-start(bf16[257,8,128]{2,1,0:T(8,128)(2,1)} %copy.26), channel_id=1, source_target_pairs={{1,0},{2,1},{3,2},{5,4},{6,5},{7,6},{9,8},{10,9},{11,10},{13,12},{... | collective-permute-start | bytes 1579016 | tf_op jit(solution)/shard_map/ppermute | solution.py:23
  24.6 47.7 %collective-permute-start.1 = (bf16[257,8,128]{2,1,0:T(8,128)(2,1)S(1)}, bf16[257,8,128]{2,1,0:T(8,128)(2,1)}, u32[]{:S(2)}, u32[]{:S(2)}) collective-permute-start(bf16[257,8,128]{2,1,0:T(8,128)(2,1)S(1)} %copy.25), channel_id=1, source_target_pairs={{0,1},{1,2},{2,3},{4,5},{5,6},{6,7},{8,9},{9,10},{10,11},{12,13},{... | collective-permute-start | bytes 1579016 | tf_op jit(solution)/shard_map/ppermute | solution.py:20
  38.1 0.5 copy-start.7
  89.8 16.8 %copy-start.4 = (bf16[64,32,128]{2,1,0:T(8,128)(2,1)S(1)}, bf16[64,32,128]{2,1,0:T(8,128)(2,1)}, u32[]{:S(2)}) copy-start(bf16[64,32,128]{2,1,0:T(8,128)(2,1)} %param.15) | copy-start | bytes 1572868
Sparse Core Ops, SparseCore 0:
  17.1 19.7 reduce-scatter.1
where the time goes:
time: 121 us
  blocking collectives  27.4 us (23%)
  matrix products  26 us (21%)
  local copies, waits for them, and re-layouts  21.4 us (18%)
  between operations  14.3 us (12%)
  other arithmetic  12.8 us (11%)
  starting transfers between devices  10.1 us (8%)
  waiting for transfers between devices  8.52 us (7%)
    unnamed x1, blocking collectives  22 us
    dot_general x1, matrix products, local(): jnp.einsum('cjte,lcjef->ctlf', picked, near_blocks, preferred_element_typ...  16.8 us
    gather x1, local copies, waits for them, and re-layouts, local(): jnp.take(cluster_major, local_index, axis=0)  12.1 us
    reduce_scatter x1, waiting for transfers between devices, local(): lax.psum_scatter(partial_moments.astype(jnp.bfloat16), 'space', scatter_d...  8.5 us
    all_gather x1, blocking collectives, local(): scaled = lax.all_gather(scaled, 'space', axis=1, tiled=True)  5.37 us
    ppermute x1, starting transfers between devices, shifted(): return lax.ppermute(block, axis, route)  4.9 us
    dot_general x1, matrix products, local(): jnp.dot(scaled, from_moments.reshape(terms, clusters_here * unknowns), pr...  4.44 us
    transpose x1, other arithmetic, local(): cluster_major = jnp.transpose(window, (1, 0, 2))  4.17 us
  transfers between devices with their start and end apart: 4, of which 1 were waited for; matrix products, arithmetic and copies ran while one was open for 12% of the time, Pallas kernels for 0%

commit v1 on v0

v1 whole, which is shorter than its diff:
```python
import functools

import jax
import jax.numpy as jnp
from jax import lax
from jax.experimental import pallas as pl
from jax.experimental.pallas import tpu as pltpu
from jax.sharding import PartitionSpec as P

REACH = 8
PAD = 16
MESH = pl.DeviceIdType.MESH
F32, BF16 = jnp.float32, jnp.bfloat16


def spread(row):
    return jnp.broadcast_to(row, (128, row.shape[1])).T


def kernel(n_tm, n_space, dens, active, nbrs, blocks, to_m, from_m, rates, lengths, out,
           dens_v, flat, work, halo, halo_prev, row_out, row_in, wb, to_raw, from_raw, to_v, from_v,
           near, stage, out_v, act, part_out, part_in, keep, tot_out, tot_in, state,
           in_sem, w_sem, halo_sem, row_sem, part_ssem, part_rsem, tot_ssem, tot_rsem, out_sem):
    T, C, E = dens_v.shape
    M = to_raw.shape[0]
    J = wb.shape[2]
    H = T // 2
    tm, sp = lax.axis_index("tm"), lax.axis_index("space")
    first = sp * C

    c_dens = pltpu.make_async_copy(dens, dens_v, in_sem.at[0])
    c_to = pltpu.make_async_copy(to_m, to_raw, in_sem.at[1])
    c_from = pltpu.make_async_copy(from_m, from_raw, in_sem.at[2])
    c_dens.start()
    c_to.start()
    c_from.start()
    barrier = pltpu.get_barrier_semaphore()

    def greet(t, s):
        pl.semaphore_signal(barrier, inc=1, device_id={"tm": t, "space": s}, device_id_type=MESH)

    for d in range(1, n_space):
        greet(tm, lax.rem(sp + d, n_space))
    for d in range(1, n_tm):
        greet(lax.rem(tm + d, n_tm), sp)
    one, nil = jnp.int32(1), jnp.int32(0)
    has = {-1: (tm > 0, sp > 0), 1: (tm < n_tm - 1, sp < n_space - 1)}
    corners = nil
    for dt in (-1, 1):
        for ds in (-1, 1):
            there = jnp.logical_and(has[dt][0], has[ds][1])
            corners = corners + jnp.where(there, one, nil)

            @pl.when(there)
            def _(dt=dt, ds=ds):
                greet(tm + dt, sp + ds)

    def w_copy(c):
        return pltpu.make_async_copy(blocks.at[:, c], wb.at[:, c], w_sem.at[c])

    for lo, hi in ((REACH, C - REACH), (0, REACH), (C - REACH, C)):
        @pl.loop(lo, hi)
        def _(c):
            w_copy(c).start()

    for h in range(2):
        act[h * H:(h + 1) * H, :] = spread(active[h:h + 1, :].astype(F32))

    c_dens.wait()
    gid = lax.broadcasted_iota(jnp.int32, (C, E), 0).astype(F32) + first.astype(F32)
    row_out[...] = jnp.where(gid < act[T - 1:T, :], dens_v[T - 1].astype(F32), 0.0)
    pl.semaphore_wait(barrier, n_space - 1 + n_tm - 1 + corners)

    def row_copy(ds):
        if ds == 0:
            src, dst = row_out, row_in.at[pl.ds(REACH, C)]
        elif ds == 1:
            src, dst = row_out.at[pl.ds(C - REACH, REACH)], row_in.at[pl.ds(0, REACH)]
        else:
            src, dst = row_out.at[pl.ds(0, REACH)], row_in.at[pl.ds(REACH + C, REACH)]
        return pltpu.make_async_remote_copy(
            src_ref=src, dst_ref=dst, send_sem=row_sem.at[0, ds + 1], recv_sem=row_sem.at[1, ds + 1],
            device_id={"tm": tm + 1, "space": sp + ds}, device_id_type=MESH)

    def halo_copy(ds):
        k = (1 - ds) // 2
        src = dens_v.at[:, pl.ds(C - REACH if ds == 1 else 0, REACH), :]
        return pltpu.make_async_remote_copy(
            src_ref=src, dst_ref=halo.at[k], send_sem=halo_sem.at[0, k], recv_sem=halo_sem.at[1, k],
            device_id={"tm": tm, "space": sp + ds}, device_id_type=MESH)

    def on_space(ds):
        return True if ds == 0 else has[ds][1]

    for ds in (0, 1, -1):
        @pl.when(jnp.logical_and(has[1][0], on_space(ds)))
        def _(ds=ds):
            row_copy(ds).start()
    for ds in (1, -1):
        @pl.when(on_space(ds))
        def _(ds=ds):
            halo_copy(ds).start()

    TB = 16
    @pl.loop(0, T // TB)
    def _(i):
        x = dens_v[pl.ds(i * TB, TB)].astype(F32)
        flat[pl.ds(pl.multiple_of(i * TB * C, TB * C), TB * C), :] = x.reshape(TB * C, E)

    @pl.loop(0, C)
    def _(g):
        x = flat[pl.ds(g, T, stride=C), :]
        live = (first + g).astype(F32) < act[...]
        work[REACH + g, 0:T, :] = jnp.where(live, x, 0.0).astype(BF16)

    def expand(raw, dst):
        @pl.loop(0, M // TB)
        def _(i):
            x = raw[pl.ds(i * TB, TB)].astype(F32)
            flat[pl.ds(pl.multiple_of(i * TB * C, TB * C), TB * C), :] = x.reshape(TB * C, E)

        @pl.loop(0, C)
        def _(g):
            x = flat[pl.ds(g, M, stride=C), :].astype(BF16)
            dst[g, 0:M, :] = x
            dst[g, M:2 * M, :] = x

    c_to.wait()
    expand(to_raw, to_v)

    lane = lax.broadcasted_iota(jnp.int32, (H, 2 * M), 1)
    low = lane < M
    total = jnp.zeros((T, 2 * M), F32)
    GB = 8
    for k in range(C // GB):
        a = jnp.concatenate([work[REACH + k * GB + i, 0:T, :] for i in range(GB)], axis=1)
        b = jnp.concatenate([to_v[k * GB + i] for i in range(GB)], axis=1)
        total = total + lax.dot_general(a, b, (((1,), (1,)), ((), ())), preferred_element_type=F32)
    part = jnp.where(low, total[0:H], total[H:T])
    keep[0] = part
    part_out[...] = part.astype(BF16)

    def part_copy(d):
        return pltpu.make_async_remote_copy(
            src_ref=part_out, dst_ref=part_in.at[sp], send_sem=part_ssem.at[d], recv_sem=part_rsem.at[sp],
            device_id={"tm": tm, "space": lax.rem(sp + d, n_space)}, device_id_type=MESH)

    for d in range(1, n_space):
        part_copy(d).start()

    c_from.wait()
    expand(from_raw, from_v)

    @pl.when(tm == 0)
    def _():
        row_in[...] = jnp.zeros_like(row_in)

    for ds in (0, 1, -1):
        there = has[-1][0] if ds == 0 else jnp.logical_and(has[-1][0], has[-ds][1])

        @pl.when(there)
        def _(ds=ds):
            row_copy(ds).wait_recv()
    top = lax.broadcasted_iota(jnp.int32, (PAD, E), 0) == 0

    @pl.loop(0, C + 2 * REACH)
    def _(g):
        r = jnp.broadcast_to(row_in[pl.ds(g, 1), :], (PAD, E))
        work[g, T:T + PAD, :] = jnp.where(top, r, 0.0).astype(BF16)

    first_row = lax.broadcasted_iota(jnp.int32, (T, E), 0) == 0

    def near_field(c):
        w_copy(c).wait()
        rows = [jnp.clip(nbrs[j, c] - first + REACH, 0, C + 2 * REACH - 1) for j in range(J)]
        picked = jnp.concatenate([work[i] for i in rows], axis=1)
        w = jnp.concatenate([wb[0, c].reshape(J * E, E), wb[1, c].reshape(J * E, E)], axis=1)
        both = jnp.dot(picked, w, preferred_element_type=F32)
        late = both[:, E:]
        late = jnp.where(first_row, late[T:T + 1, :], pltpu.roll(late[0:T], 1, 0))
        near[c] = both[0:T, 0:E] + late

    pl.loop(REACH, C - REACH)(near_field)

    moment = keep[0]
    for d in range(1, n_space):
        k = lax.rem(sp + n_space - d, n_space)
        pltpu.make_async_remote_copy(
            src_ref=part_out, dst_ref=part_in.at[k], send_sem=part_ssem.at[d], recv_sem=part_rsem.at[k],
            device_id={"tm": tm, "space": k}, device_id_type=MESH).wait_recv()
        moment = moment + part_in[k].astype(F32)
    r = rates[...]
    rr = jnp.concatenate([r, r], axis=1)
    span = jnp.where(low, spread(lengths[0:1, :]), spread(lengths[1:2, :]))
    fall = jnp.exp(-rr * span)
    pos = lax.broadcasted_iota(jnp.int32, (H, 2 * M), 0)
    d = 1
    while d < H:
        start = pos < d
        moment = fall * jnp.where(start, 0.0, pltpu.roll(moment, d, 0)) + moment
        fall = fall * jnp.where(start, 1.0, pltpu.roll(fall, d, 0))
        d *= 2
    keep[0] = jnp.where(pos < 1, 0.0, pltpu.roll(moment, 1, 0))
    keep[1] = jnp.where(pos < 1, 1.0, pltpu.roll(fall, 1, 0))
    end_b = jnp.broadcast_to(moment[H - 1:H, :], (8, 2 * M))
    end_a = jnp.broadcast_to(fall[H - 1:H, :], (8, 2 * M))
    low8 = low[0:8]
    roll_b, roll_a = pltpu.roll(end_b, M, 1), pltpu.roll(end_a, M, 1)
    tot_out[0:8] = end_a * roll_a
    tot_out[8:16] = jnp.where(low8, roll_a * end_b + roll_b, end_a * roll_b + end_b)

    def tot_copy(d):
        return pltpu.make_async_remote_copy(
            src_ref=tot_out, dst_ref=tot_in.at[tm], send_sem=tot_ssem.at[d], recv_sem=tot_rsem.at[tm],
            device_id={"tm": tm + d, "space": sp}, device_id_type=MESH)

    for d in range(1, n_tm):
        @pl.when(tm + d < n_tm)
        def _(d=d):
            tot_copy(d).start()

    for ds in (1, -1):
        k = (1 - ds) // 2

        @pl.when(on_space(-ds))
        def _(ds=ds, k=k):
            halo_copy(ds).wait_recv()

            @pl.loop(0, T // 32)
            def _(i):
                x = halo[k, pl.ds(i * 32, 32)].astype(F32)
                flat[pl.ds(pl.multiple_of(i * 32 * REACH, 32 * REACH), 32 * REACH), :] = x.reshape(32 * REACH, E)

            begin = 0 if k == 0 else REACH + C

            @pl.loop(0, REACH)
            def _(g):
                x = flat[pl.ds(g, T, stride=REACH), :]
                live = (first - REACH + begin + g).astype(F32) < act[...]
                work[begin + g, 0:T, :] = jnp.where(live, x, 0.0).astype(BF16)

    @pl.loop(0, 2 * REACH)
    def _(i):
        near_field(jnp.where(i < REACH, i, i + C - 2 * REACH))

    state[...] = jnp.zeros_like(state)
    for k in range(n_tm - 1):
        @pl.when(k < tm)
        def _(k=k):
            pltpu.make_async_remote_copy(
                src_ref=tot_out, dst_ref=tot_in.at[k], send_sem=tot_ssem.at[0], recv_sem=tot_rsem.at[k],
                device_id={"tm": jnp.int32(k), "space": sp}, device_id_type=MESH).wait_recv()
            state[...] = tot_in[k, 0:8] * state[...] + tot_in[k, 8:16]
    s = state[...]
    arrive = jnp.where(low8, s, roll_a * s + roll_b)[0:1]
    scaled = (keep[1] * arrive + keep[0]) * jnp.sqrt(2.0 * rr)
    scaled = jnp.concatenate([jnp.where(low, scaled, 0.0), jnp.where(low, 0.0, scaled)], axis=0).astype(BF16)

    def out_copy(k):
        return pltpu.make_async_copy(out_v.at[k], out.at[:, pl.ds(k * GB, GB), :], out_sem.at[k])

    for k in range(C // GB):
        for i in range(0, GB, 2):
            g = k * GB + i
            far = jnp.dot(scaled, jnp.concatenate([from_v[g], from_v[g + 1]], axis=1), preferred_element_type=F32)
            for u in range(2):
                live = (first + g + u).astype(F32) < act[...]
                pot = jnp.where(live, near[g + u] + far[:, u * E:(u + 1) * E], 0.0)
                stage[pl.ds(i + u, T, stride=GB), :] = pot
        out_v[k] = stage[...].reshape(T, GB, E).astype(BF16)
        out_copy(k).start()

    for k in range(C // GB):
        out_copy(k).wait()
    for d in range(1, n_space):
        part_copy(d).wait_send()
    for d in range(1, n_tm):
        @pl.when(tm + d < n_tm)
        def _(d=d):
            tot_copy(d).wait_send()
    for ds in (0, 1, -1):
        @pl.when(jnp.logical_and(has[1][0], on_space(ds)))
        def _(ds=ds):
            row_copy(ds).wait_send()
    for ds in (1, -1):
        @pl.when(on_space(ds))
        def _(ds=ds):
            halo_copy(ds).wait_send()


def solution(mesh):
    n_tm, n_space = mesh.shape["tm"], mesh.shape["space"]

    def local(density, active, neighbours, near_blocks, to_moments, from_moments, decay_rates, lengths):
        T, C, E = density.shape
        J = neighbours.shape[1]
        M = decay_rates.shape[0]
        H, W = T // 2, C + 2 * REACH
        vm = lambda shape, t: pltpu.VMEM(shape, t)
        dma = pltpu.SemaphoreType.DMA
        anyspec = pl.BlockSpec(memory_space=pl.ANY)
        vspec = pl.BlockSpec(memory_space=pltpu.VMEM)
        return pl.pallas_call(
            functools.partial(kernel, n_tm, n_space),
            out_shape=jax.ShapeDtypeStruct((T, C, E), BF16),
            in_specs=[anyspec, vspec, pl.BlockSpec(memory_space=pltpu.SMEM), anyspec, anyspec, anyspec, vspec, vspec],
            out_specs=anyspec,
            scratch_shapes=[
                vm((T, C, E), BF16), vm((T * C, E), F32), vm((W, T + PAD, E), BF16),
                vm((2, T, REACH, E), BF16), vm((8, 128), F32), vm((C, E), F32), vm((W, E), F32),
                vm((2, C, J, E, E), BF16), vm((M, C, E), BF16), vm((M, C, E), BF16),
                vm((C, 2 * M, E), BF16), vm((C, 2 * M, E), BF16),
                vm((C, T, E), F32), vm((T * 8, E), F32), vm((C // 8, T, 8, E), BF16), vm((T, 128), F32),
                vm((H, 2 * M), BF16), vm((n_space, H, 2 * M), BF16), vm((2, H, 2 * M), F32),
                vm((16, 2 * M), F32), vm((n_tm, 16, 2 * M), F32), vm((8, 2 * M), F32),
                dma((3,)), dma((C,)), dma((2, 2)), dma((2, 3)), dma((n_space,)), dma((n_space,)),
                dma((n_tm,)), dma((n_tm,)), dma((C // 8,)),
            ],
            compiler_params=pltpu.CompilerParams(
                collective_id=0, has_side_effects=True, vmem_limit_bytes=60 * 1024 * 1024),
        )(density, active.reshape(2, H), neighbours.T, near_blocks, to_moments, from_moments,
          decay_rates.reshape(1, M), lengths.reshape(2, H))

    placed = (
        P("tm", "space", None), P("tm"), P("space", None), P(None, "space", None, None, None),
        P(None, "space", None), P(None, "space", None), P(), P("tm"),
    )
    return jax.shard_map(
        local, mesh=mesh, in_specs=placed, out_specs=P("tm", "space", None), check_vma=False)
```

time: 121 us -> 32.8 us (0.27)
  Pallas kernels: 0 us -> 29.4 us
  blocking collectives: 27.4 us -> 0 us
  matrix products: 26 us -> 0 us
  local copies, waits for them, and re-layouts: 21.4 us -> 3.27 us
  between operations: 14.3 us -> 0.01 us
  other arithmetic: 12.8 us -> 0 us
  starting transfers between devices: 10.1 us -> 0 us
  waiting for transfers between devices: 8.52 us -> 0 us
    pallas_call x0 -> x1, Pallas kernels: none -> 29.4 us  [local(): pl.pallas_call(functools.partial(kernel, n_tm, n_space), out_shape=jax.Sh...]
    dot_general x4 -> x0, matrix products: 26 us -> none  [the longest x1 16.8 us: local(): jnp.einsum('cjte,lcjef->ctlf', picked, near_blocks, preferred_element_typ...]
    unnamed x1 -> x0, blocking collectives: 22 us -> none
    gather x1 -> x0, local copies, waits for them, and re-layouts: 12.1 us -> none  [local(): jnp.take(cluster_major, local_index, axis=0)]
    ppermute x3 -> x0, starting transfers between devices: 10 us -> none  [the longest x1 4.9 us: shifted(): return lax.ppermute(block, axis, route)]
    reduce_scatter x1 -> x0, waiting for transfers between devices: 8.5 us -> none  [local(): lax.psum_scatter(partial_moments.astype(jnp.bfloat16), 'space', scatter_d...]
    all_gather x1 -> x0, blocking collectives: 5.37 us -> none  [local(): scaled = lax.all_gather(scaled, 'space', axis=1, tiled=True)]
    transpose x1 -> x0, other arithmetic: 4.17 us -> none  [local(): cluster_major = jnp.transpose(window, (1, 0, 2))]
  transfers between devices with their start and end apart: 4 -> 0, of which waited for: 1 -> 0; matrix products, arithmetic and copies ran while one was open for 12% -> 0% of each run, Pallas kernels for 0% -> 0%
where the time goes in v1:
time: 32.8 us; the launch traced here: 32.6 us
  Pallas kernels  29.4 us (90%)
  local copies, waits for them, and re-layouts  3.27 us (10%)
    pallas_call x1, Pallas kernels, local(): pl.pallas_call(functools.partial(kernel, n_tm, n_space), out_shape=jax.Sh...  29.4 us
    unnamed x1, local copies, waits for them, and re-layouts  3.27 us

profile of v1, /device:TPU:0, one launch (start us, length us, event | category | flops | bytes accessed | tf_op | source)
XLA Modules:
  0.0 32.6 jit_solution(3746759331503397464)
XLA Ops:
  0.0 29.4 %shard_map.82 = bf16[256,32,128]{2,1,0:T(8,128)(2,1)} custom-call(bf16[256,32,128]{2,1,0:T(8,128)(2,1)} %dens.1, s32[2,128]{1,0:T(2,128)} %bitcast.5, s32[8,32]{1,0:T(8,128)} %bitcast.4, bf16[2,32,8,128,128]{4,3,2,1,0:T(8,128)(2,1)} %blocks.1, bf16[64,32,128]{2,1,0:T(8,128)(2,1)} %to_m.1, bf16[64,32,128]{2,1,0:T(8,128)(2,1)} %from_m.1, f32[1,64]{1,0:T(1,128)} %bitcast.7, ...), custom_call_target="tpu_custom_call" | custom-call | tf_op jit(solution)/shard_map/pallas_call | solution.py:303
  29.4 3.3 %copy.10 = bf16[256,32,128]{2,1,0:T(8,128)(2,1)} copy(bf16[256,32,128]{2,1,0:T(8,128)(2,1)} %shard_map.82) | data formatting | bytes 4194304

commit v2 on v1

--- a/solution.py
+++ b/solution.py
@@ -1,4 +1,5 @@
 import functools
+import math
 
 import jax
 import jax.numpy as jnp
@@ -9,6 +10,7 @@
 
 REACH = 8
 PAD = 16
+VMEM = 67043328
 MESH = pl.DeviceIdType.MESH
 F32, BF16 = jnp.float32, jnp.bfloat16
 
@@ -17,10 +19,10 @@
     return jnp.broadcast_to(row, (128, row.shape[1])).T
 
 
-def kernel(n_tm, n_space, dens, active, nbrs, blocks, to_m, from_m, rates, lengths, out,
-           dens_v, flat, work, halo, halo_prev, row_out, row_in, wb, to_raw, from_raw, to_v, from_v,
-           near, stage, out_v, act, part_out, part_in, keep, tot_out, tot_in, state,
-           in_sem, w_sem, halo_sem, row_sem, part_ssem, part_rsem, tot_ssem, tot_rsem, out_sem):
+def kernel(n_tm, n_space, dens, active, nbrs, blocks, to_m, from_m, rates, lengths,
+           near, from_v, act, scaled_o, dens_v, flat, work, halo, halo_prev, row_out, row_in, wb, to_raw, from_raw, to_v,
+           part_out, part_in, keep, tot_out, tot_in, state,
+           in_sem, w_sem, halo_sem, row_sem, part_ssem, part_rsem, tot_ssem, tot_rsem):
     T, C, E = dens_v.shape
     M = to_raw.shape[0]
     J = wb.shape[2]
@@ -33,7 +35,6 @@
     c_from = pltpu.make_async_copy(from_m, from_raw, in_sem.at[2])
     c_dens.start()
     c_to.start()
-    c_from.start()
     barrier = pltpu.get_barrier_semaphore()
 
     def greet(t, s):
@@ -58,15 +59,16 @@
     def w_copy(c):
         return pltpu.make_async_copy(blocks.at[:, c], wb.at[:, c], w_sem.at[c])
 
+    for h in range(2):
+        act[h * H:(h + 1) * H, :] = spread(active[h:h + 1, :].astype(F32))
+
+    c_dens.wait()
+    c_from.start()
     for lo, hi in ((REACH, C - REACH), (0, REACH), (C - REACH, C)):
         @pl.loop(lo, hi)
         def _(c):
             w_copy(c).start()
 
-    for h in range(2):
-        act[h * H:(h + 1) * H, :] = spread(active[h:h + 1, :].astype(F32))
-
-    c_dens.wait()
     gid = lax.broadcasted_iota(jnp.int32, (C, E), 0).astype(F32) + first.astype(F32)
     row_out[...] = jnp.where(gid < act[T - 1:T, :], dens_v[T - 1].astype(F32), 0.0)
     pl.semaphore_wait(barrier, n_space - 1 + n_tm - 1 + corners)
@@ -102,26 +104,31 @@
             halo_copy(ds).start()
 
     TB = 16
-    @pl.loop(0, T // TB)
-    def _(i):
-        x = dens_v[pl.ds(i * TB, TB)].astype(F32)
-        flat[pl.ds(pl.multiple_of(i * TB * C, TB * C), TB * C), :] = x.reshape(TB * C, E)
+
+    def group(raw, n):
+        @pl.loop(0, n // TB)
+        def _(i):
+            x = raw[pl.ds(i * TB, TB)].astype(F32)
+            for q in range(C // 8):
+                at = pl.multiple_of(q * n * 8 + i * TB * 8, TB * 8)
+                flat[pl.ds(at, TB * 8), :] = x[:, q * 8:q * 8 + 8].reshape(TB * 8, E)
+
+    def cluster(g, n):
+        return flat[pl.ds(g // 8 * (n * 8) + g % 8, n, stride=8), :]
+
+    group(dens_v, T)
 
     @pl.loop(0, C)
     def _(g):
-        x = flat[pl.ds(g, T, stride=C), :]
         live = (first + g).astype(F32) < act[...]
-        work[REACH + g, 0:T, :] = jnp.where(live, x, 0.0).astype(BF16)
+        work[REACH + g, 0:T, :] = jnp.where(live, cluster(g, T), 0.0).astype(BF16)
 
     def expand(raw, dst):
-        @pl.loop(0, M // TB)
-        def _(i):
-            x = raw[pl.ds(i * TB, TB)].astype(F32)
-            flat[pl.ds(pl.multiple_of(i * TB * C, TB * C), TB * C), :] = x.reshape(TB * C, E)
+        group(raw, M)
 
         @pl.loop(0, C)
         def _(g):
-            x = flat[pl.ds(g, M, stride=C), :].astype(BF16)
+            x = cluster(g, M).astype(BF16)
             dst[g, 0:M, :] = x
             dst[g, M:2 * M, :] = x
 
@@ -254,7 +261,31 @@
     s = state[...]
     arrive = jnp.where(low8, s, roll_a * s + roll_b)[0:1]
     scaled = (keep[1] * arrive + keep[0]) * jnp.sqrt(2.0 * rr)
-    scaled = jnp.concatenate([jnp.where(low, scaled, 0.0), jnp.where(low, 0.0, scaled)], axis=0).astype(BF16)
+    scaled_o[0:H] = jnp.where(low, scaled, 0.0).astype(BF16)
+    scaled_o[H:T] = jnp.where(low, 0.0, scaled).astype(BF16)
+
+
+    for d in range(1, n_space):
+        part_copy(d).wait_send()
+    for d in range(1, n_tm):
+        @pl.when(tm + d < n_tm)
+        def _(d=d):
+            tot_copy(d).wait_send()
+    for ds in (0, 1, -1):
+        @pl.when(jnp.logical_and(has[1][0], on_space(ds)))
+        def _(ds=ds):
+            row_copy(ds).wait_send()
+    for ds in (1, -1):
+        @pl.when(on_space(ds))
+        def _(ds=ds):
+            halo_copy(ds).wait_send()
+
+
+def finish(near, from_v, act, scaled_o, out, stage, out_v, out_sem):
+    C, T, E = near.shape
+    GB = 8
+    first = lax.axis_index("space") * C
+    scaled = scaled_o[...]
 
     def out_copy(k):
         return pltpu.make_async_copy(out_v.at[k], out.at[:, pl.ds(k * GB, GB), :], out_sem.at[k])
@@ -269,23 +300,8 @@
                 stage[pl.ds(i + u, T, stride=GB), :] = pot
         out_v[k] = stage[...].reshape(T, GB, E).astype(BF16)
         out_copy(k).start()
-
     for k in range(C // GB):
         out_copy(k).wait()
-    for d in range(1, n_space):
-        part_copy(d).wait_send()
-    for d in range(1, n_tm):
-        @pl.when(tm + d < n_tm)
-        def _(d=d):
-            tot_copy(d).wait_send()
-    for ds in (0, 1, -1):
-        @pl.when(jnp.logical_and(has[1][0], on_space(ds)))
-        def _(ds=ds):
-            row_copy(ds).wait_send()
-    for ds in (1, -1):
-        @pl.when(on_space(ds))
-        def _(ds=ds):
-            halo_copy(ds).wait_send()
 
 
 def solution(mesh):
@@ -298,28 +314,37 @@
         H, W = T // 2, C + 2 * REACH
         vm = lambda shape, t: pltpu.VMEM(shape, t)
         dma = pltpu.SemaphoreType.DMA
+        kept = [((C, T, E), F32), ((C, 2 * M, E), BF16), ((T, 128), F32), ((T, 2 * M), BF16)]
+        room = sum(math.prod(s) * jnp.dtype(t).itemsize for s, t in kept) + 32 * 1024
         anyspec = pl.BlockSpec(memory_space=pl.ANY)
         vspec = pl.BlockSpec(memory_space=pltpu.VMEM)
-        return pl.pallas_call(
+        held = pl.pallas_call(
             functools.partial(kernel, n_tm, n_space),
-            out_shape=jax.ShapeDtypeStruct((T, C, E), BF16),
+            out_shape=[pltpu.VMEM(s, t) for s, t in kept],
             in_specs=[anyspec, vspec, pl.BlockSpec(memory_space=pltpu.SMEM), anyspec, anyspec, anyspec, vspec, vspec],
-            out_specs=anyspec,
+            out_specs=[vspec] * 4,
             scratch_shapes=[
                 vm((T, C, E), BF16), vm((T * C, E), F32), vm((W, T + PAD, E), BF16),
                 vm((2, T, REACH, E), BF16), vm((8, 128), F32), vm((C, E), F32), vm((W, E), F32),
                 vm((2, C, J, E, E), BF16), vm((M, C, E), BF16), vm((M, C, E), BF16),
-                vm((C, 2 * M, E), BF16), vm((C, 2 * M, E), BF16),
-                vm((C, T, E), F32), vm((T * 8, E), F32), vm((C // 8, T, 8, E), BF16), vm((T, 128), F32),
+                vm((C, 2 * M, E), BF16),
                 vm((H, 2 * M), BF16), vm((n_space, H, 2 * M), BF16), vm((2, H, 2 * M), F32),
                 vm((16, 2 * M), F32), vm((n_tm, 16, 2 * M), F32), vm((8, 2 * M), F32),
                 dma((3,)), dma((C,)), dma((2, 2)), dma((2, 3)), dma((n_space,)), dma((n_space,)),
-                dma((n_tm,)), dma((n_tm,)), dma((C // 8,)),
+                dma((n_tm,)), dma((n_tm,)),
             ],
             compiler_params=pltpu.CompilerParams(
-                collective_id=0, has_side_effects=True, vmem_limit_bytes=60 * 1024 * 1024),
+                collective_id=0, has_side_effects=True, vmem_limit_bytes=VMEM - room),
         )(density, active.reshape(2, H), neighbours.T, near_blocks, to_moments, from_moments,
           decay_rates.reshape(1, M), lengths.reshape(2, H))
+        return pl.pallas_call(
+            finish,
+            out_shape=jax.ShapeDtypeStruct((T, C, E), BF16),
+            in_specs=[vspec] * 4,
+            out_specs=anyspec,
+            scratch_shapes=[vm((T * 8, E), F32), vm((C // 8, T, 8, E), BF16), dma((C // 8,))],
+            compiler_params=pltpu.CompilerParams(vmem_limit_bytes=16 * 1024 * 1024),
+        )(*held)
 
     placed = (
         P("tm", "space", None), P("tm"), P("space", None), P(None, "space", None, None, None),

time: 32.8 us -> 25.5 us (0.78)
  Pallas kernels: 29.4 us -> 25.1 us
  local copies, waits for them, and re-layouts: 3.27 us -> 0 us
    pallas_call x1 -> x2, Pallas kernels: 29.4 us -> 25.1 us  [the longest x1 23.2 us: local(): pl.pallas_call(functools.partial(kernel, n_tm, n_space), out_shape=[pltpu...]
    unnamed x1 -> x0, local copies, waits for them, and re-layouts: 3.27 us -> none
where the time goes in v2:
time: 25.5 us; the launch traced here: 25.1 us
  Pallas kernels  25.1 us (98%)
    pallas_call x1, Pallas kernels, local(): pl.pallas_call(functools.partial(kernel, n_tm, n_space), out_shape=[pltpu...  23.2 us
    pallas_call x1, Pallas kernels, local(): pl.pallas_call(finish, out_shape=jax.ShapeDtypeStruct((T, C, E), BF16), i...  1.94 us

profile of v2, /device:TPU:0, one launch (start us, length us, event | category | flops | bytes accessed | tf_op | source)
XLA Modules:
  0.0 25.1 jit_solution(2065050888863166453)
XLA Ops:
  0.0 23.2 %shard_map.82 = (f32[32,256,128]{2,1,0:T(8,128)S(1)}, bf16[32,128,128]{2,1,0:T(8,128)(2,1)S(1)}, f32[256,128]{1,0:T(8,128)S(1)}, bf16[256,128]{1,0:T(8,128)(2,1)S(1)}) custom-call(bf16[256,32,128]{2,1,0:T(8,128)(2,1)} %dens.1, s32[2,128]{1,0:T(2,128)} %bitcast.5, s32[8,32]{1,0:T(8,128)} %bitcast.4, bf16[2,32,8,128,128]{4,3,2,1,0:T(8,128)(2,1)} %blocks.1, ...), custom_call_target="tpu_custom_call" | custom-call | tf_op jit(solution)/shard_map/pallas_call | solution.py:321
  23.2 1.9 %shard_map.83 = bf16[256,32,128]{2,1,0:T(8,128)(2,1)} custom-call(f32[32,256,128]{2,1,0:T(8,128)S(1)} %get-tuple-element.9.near, bf16[32,128,128]{2,1,0:T(8,128)(2,1)S(1)} %get-tuple-element.10.from_v, f32[256,128]{1,0:T(8,128)S(1)} %get-tuple-element.11.act, bf16[256,128]{1,0:T(8,128)(2,1)S(1)} %get-tuple-element.12.scaled_o), custom_call_target="tpu_custom_call" | custom-call | tf_op jit(solution)/shard_map/pallas_call | solution.py:340

commit v3 on v2

--- a/solution.py
+++ b/solution.py
@@ -33,8 +33,9 @@
     c_dens = pltpu.make_async_copy(dens, dens_v, in_sem.at[0])
     c_to = pltpu.make_async_copy(to_m, to_raw, in_sem.at[1])
     c_from = pltpu.make_async_copy(from_m, from_raw, in_sem.at[2])
+    c_to.start()
     c_dens.start()
-    c_to.start()
+    c_from.start()
     barrier = pltpu.get_barrier_semaphore()
 
     def greet(t, s):
@@ -62,8 +63,31 @@
     for h in range(2):
         act[h * H:(h + 1) * H, :] = spread(active[h:h + 1, :].astype(F32))
 
+    TB = 16
+
+    def group(raw, n):
+        @pl.loop(0, n // TB)
+        def _(i):
+            x = raw[pl.ds(i * TB, TB)].astype(F32)
+            for q in range(C // 8):
+                at = pl.multiple_of(q * n * 8 + i * TB * 8, TB * 8)
+                flat[pl.ds(at, TB * 8), :] = x[:, q * 8:q * 8 + 8].reshape(TB * 8, E)
+
+    def cluster(g, n):
+        return flat[pl.ds(g // 8 * (n * 8) + g % 8, n, stride=8), :]
+
+    def expand(raw, dst):
+        group(raw, M)
+
+        @pl.loop(0, C)
+        def _(g):
+            x = cluster(g, M).astype(BF16)
+            dst[g, 0:M, :] = x
+            dst[g, M:2 * M, :] = x
+
+    c_to.wait()
+    expand(to_raw, to_v)
     c_dens.wait()
-    c_from.start()
     for lo, hi in ((REACH, C - REACH), (0, REACH), (C - REACH, C)):
         @pl.loop(lo, hi)
         def _(c):
@@ -71,6 +95,8 @@
 
     gid = lax.broadcasted_iota(jnp.int32, (C, E), 0).astype(F32) + first.astype(F32)
     row_out[...] = jnp.where(gid < act[T - 1:T, :], dens_v[T - 1].astype(F32), 0.0)
+    c_from.wait()
+    expand(from_raw, from_v)
     pl.semaphore_wait(barrier, n_space - 1 + n_tm - 1 + corners)
 
     def row_copy(ds):
@@ -84,12 +110,19 @@
             src_ref=src, dst_ref=dst, send_sem=row_sem.at[0, ds + 1], recv_sem=row_sem.at[1, ds + 1],
             device_id={"tm": tm + 1, "space": sp + ds}, device_id_type=MESH)
 
-    def halo_copy(ds):
+    def halo_copy(ds, h):
         k = (1 - ds) // 2
-        src = dens_v.at[:, pl.ds(C - REACH if ds == 1 else 0, REACH), :]
         return pltpu.make_async_remote_copy(
-            src_ref=src, dst_ref=halo.at[k], send_sem=halo_sem.at[0, k], recv_sem=halo_sem.at[1, k],
+            src_ref=dens_v.at[pl.ds(h * H, H), pl.ds(C - REACH if ds == 1 else 0, REACH), :],
+            dst_ref=halo.at[k, pl.ds(h * H, H)],
+            send_sem=halo_sem.at[0, k, h], recv_sem=halo_sem.at[1, k, h],
             device_id={"tm": tm, "space": sp + ds}, device_id_type=MESH)
+
+    def halo_send(h):
+        for ds in (1, -1):
+            @pl.when(on_space(ds))
+            def _(ds=ds):
+                halo_copy(ds, h).start()
 
     def on_space(ds):
         return True if ds == 0 else has[ds][1]
@@ -98,23 +131,7 @@
         @pl.when(jnp.logical_and(has[1][0], on_space(ds)))
         def _(ds=ds):
             row_copy(ds).start()
-    for ds in (1, -1):
-        @pl.when(on_space(ds))
-        def _(ds=ds):
-            halo_copy(ds).start()
-
-    TB = 16
-
-    def group(raw, n):
-        @pl.loop(0, n // TB)
-        def _(i):
-            x = raw[pl.ds(i * TB, TB)].astype(F32)
-            for q in range(C // 8):
-                at = pl.multiple_of(q * n * 8 + i * TB * 8, TB * 8)
-                flat[pl.ds(at, TB * 8), :] = x[:, q * 8:q * 8 + 8].reshape(TB * 8, E)
-
-    def cluster(g, n):
-        return flat[pl.ds(g // 8 * (n * 8) + g % 8, n, stride=8), :]
+    halo_send(0)
 
     group(dens_v, T)
 
@@ -122,18 +139,6 @@
     def _(g):
         live = (first + g).astype(F32) < act[...]
         work[REACH + g, 0:T, :] = jnp.where(live, cluster(g, T), 0.0).astype(BF16)
-
-    def expand(raw, dst):
-        group(raw, M)
-
-        @pl.loop(0, C)
-        def _(g):
-            x = cluster(g, M).astype(BF16)
-            dst[g, 0:M, :] = x
-            dst[g, M:2 * M, :] = x
-
-    c_to.wait()
-    expand(to_raw, to_v)
 
     lane = lax.broadcasted_iota(jnp.int32, (H, 2 * M), 1)
     low = lane < M
@@ -154,9 +159,7 @@
 
     for d in range(1, n_space):
         part_copy(d).start()
-
-    c_from.wait()
-    expand(from_raw, from_v)
+    halo_send(1)
 
     @pl.when(tm == 0)
     def _():
@@ -226,19 +229,24 @@
         def _(d=d):
             tot_copy(d).start()
 
-    for ds in (1, -1):
-        k = (1 - ds) // 2
-
-        @pl.when(on_space(-ds))
-        def _(ds=ds, k=k):
-            halo_copy(ds).wait_recv()
+    near_side = jnp.where(lax.rem(sp, 2) == 1, nil, one)
+    for k in (near_side, one - near_side):
+        other = sp + 2 * k - 1
+
+        @pl.when(jnp.logical_and(other >= 0, other < n_space))
+        def _(k=k, other=other):
+            for h in range(2):
+                pltpu.make_async_remote_copy(
+                    src_ref=dens_v.at[pl.ds(h * H, H), pl.ds(0, REACH), :], dst_ref=halo.at[k, pl.ds(h * H, H)],
+                    send_sem=halo_sem.at[0, k, h], recv_sem=halo_sem.at[1, k, h],
+                    device_id={"tm": tm, "space": other}, device_id_type=MESH).wait_recv()
 
             @pl.loop(0, T // 32)
             def _(i):
                 x = halo[k, pl.ds(i * 32, 32)].astype(F32)
                 flat[pl.ds(pl.multiple_of(i * 32 * REACH, 32 * REACH), 32 * REACH), :] = x.reshape(32 * REACH, E)
 
-            begin = 0 if k == 0 else REACH + C
+            begin = k * (REACH + C)
 
             @pl.loop(0, REACH)
             def _(g):
@@ -246,9 +254,9 @@
                 live = (first - REACH + begin + g).astype(F32) < act[...]
                 work[begin + g, 0:T, :] = jnp.where(live, x, 0.0).astype(BF16)
 
-    @pl.loop(0, 2 * REACH)
-    def _(i):
-        near_field(jnp.where(i < REACH, i, i + C - 2 * REACH))
+        @pl.loop(0, REACH)
+        def _(i):
+            near_field(i + k * (C - REACH))
 
     state[...] = jnp.zeros_like(state)
     for k in range(n_tm - 1):
@@ -278,7 +286,8 @@
     for ds in (1, -1):
         @pl.when(on_space(ds))
         def _(ds=ds):
-            halo_copy(ds).wait_send()
+            for h in range(2):
+                halo_copy(ds, h).wait_send()
 
 
 def finish(near, from_v, act, scaled_o, out, stage, out_v, out_sem):
@@ -330,7 +339,7 @@
                 vm((C, 2 * M, E), BF16),
                 vm((H, 2 * M), BF16), vm((n_space, H, 2 * M), BF16), vm((2, H, 2 * M), F32),
                 vm((16, 2 * M), F32), vm((n_tm, 16, 2 * M), F32), vm((8, 2 * M), F32),
-                dma((3,)), dma((C,)), dma((2, 2)), dma((2, 3)), dma((n_space,)), dma((n_space,)),
+                dma((3,)), dma((C,)), dma((2, 2, 2)), dma((2, 3)), dma((n_space,)), dma((n_space,)),
                 dma((n_tm,)), dma((n_tm,)),
             ],
             compiler_params=pltpu.CompilerParams(

time: 25.5 us -> 23.7 us (0.929)
  Pallas kernels: 25.1 us -> 23.5 us
    pallas_call x1, Pallas kernels: 23.2 us -> 21.6 us  [local(): pl.pallas_call(functools.partial(kernel, n_tm, n_space), out_shape=[pltpu...]
where the time goes in v3:
time: 23.7 us; the launch traced here: 23.5 us
  Pallas kernels  23.5 us (99%)
    pallas_call x1, Pallas kernels, local(): pl.pallas_call(functools.partial(kernel, n_tm, n_space), out_shape=[pltpu...  21.6 us
    pallas_call x1, Pallas kernels, local(): pl.pallas_call(finish, out_shape=jax.ShapeDtypeStruct((T, C, E), BF16), i...  1.94 us

profile of v3, /device:TPU:0, one launch (start us, length us, event | category | flops | bytes accessed | tf_op | source)
XLA Modules:
  0.0 23.5 jit_solution(17550548634797024740)
XLA Ops:
  0.0 21.6 %shard_map.82 = (f32[32,256,128]{2,1,0:T(8,128)S(1)}, bf16[32,128,128]{2,1,0:T(8,128)(2,1)S(1)}, f32[256,128]{1,0:T(8,128)S(1)}, bf16[256,128]{1,0:T(8,128)(2,1)S(1)}) custom-call(bf16[256,32,128]{2,1,0:T(8,128)(2,1)} %dens.1, s32[2,128]{1,0:T(2,128)} %bitcast.5, s32[8,32]{1,0:T(8,128)} %bitcast.4, bf16[2,32,8,128,128]{4,3,2,1,0:T(8,128)(2,1)} %blocks.1, ...), custom_call_target="tpu_custom_call" | custom-call | tf_op jit(solution)/shard_map/pallas_call | solution.py:330
  21.6 1.9 %shard_map.83 = bf16[256,32,128]{2,1,0:T(8,128)(2,1)} custom-call(f32[32,256,128]{2,1,0:T(8,128)S(1)} %get-tuple-element.9.near, bf16[32,128,128]{2,1,0:T(8,128)(2,1)S(1)} %get-tuple-element.10.from_v, f32[256,128]{1,0:T(8,128)S(1)} %get-tuple-element.11.act, bf16[256,128]{1,0:T(8,128)(2,1)S(1)} %get-tuple-element.12.scaled_o), custom_call_target="tpu_custom_call" | custom-call | tf_op jit(solution)/shard_map/pallas_call | solution.py:349
